TPU v7x, 32 devices: a whole 2x2x4 slice. The times are simulated.
32 devices in a mesh: row: 4 (over y, core), col: 8 (over z, x).
Axes of the slice: x: 2, y: 2, z: 4, core: 2. Of those that a mesh axis runs over, the one named last changes fastest.
Arguments:
- blocks: float32 [4096, 128, 128], P(('row', 'col')), may hold values from -0.25 to 0.25
- block_rows: int32 [32, 128], P(('row', 'col')), may hold values from 0 to 1023, as said below
- block_cols: int32 [32, 128], P(('row', 'col')), may hold values from 0 to 511
- diagonal: float32 [524288], P(('row', 'col')), may hold values from 1 to 4
- right_sides: float32 [2, 524288], P(None, ('row', 'col')), may hold values from -6 to 6
Outputs:
- solution: float32 [2, 524288], P(None, ('row', 'col'))
- hessenberg: float32 [2, 9, 8], replicated
Inputs may be any that keep to these rules, and one draw needn't show every extreme that they name: `block_rows`: non-decreasing along each tile's slots; a local block row may hold no stored block.
All inputs are finite; a program needn't handle non-finite values.
Results may differ from a plain program's by a relative error of at most 0.0085.
Values sent between devices are 32-bit elements; how exact they have to be, the bound alone decides.
A program may use at most 128 MiB of HBM per device.

v0:
```python
import jax
import jax.numpy as jnp
from jax import lax
from jax.sharding import PartitionSpec as P

STEPS = 8
epsilon = 1e-06


def least_squares(hessenberg, initial_norm):
    total_steps = hessenberg.shape[2]
    targets = [initial_norm] + [jnp.zeros_like(initial_norm) for j in range(total_steps)]
    cosines, sines, triangle = ([], [], [])
    for j in range(total_steps):
        column = [hessenberg[:, i, j] for i in range(j + 2)]
        for i in range(j):
            leading, trailing = (column[i], column[i + 1])
            column[i] = cosines[i] * leading + sines[i] * trailing
            column[i + 1] = cosines[i] * trailing - sines[i] * leading
        radius = jnp.sqrt(column[j] * column[j] + column[j + 1] * column[j + 1])
        cosine = column[j] / radius
        sine_term = column[j + 1] / radius
        column[j] = radius
        cosines.append(cosine)
        sines.append(sine_term)
        targets[j + 1] = -sine_term * targets[j]
        targets[j] = cosine * targets[j]
        triangle.append(column[: j + 1])
    coeffs = [None] * total_steps
    for j in reversed(range(total_steps)):
        running = targets[j]
        for k in range(j + 1, total_steps):
            running = running - triangle[k][j] * coeffs[k]
        coeffs[j] = running / triangle[j][j]
    return jnp.stack(coeffs, axis=1)


def apply_matrix(vector, blocks, rows_onehot, block_cols, diagonal):
    systems = vector.shape[0]
    width = blocks.shape[1]
    gathered = lax.all_gather(vector, "row", axis=1, tiled=True)
    grouped = gathered.reshape(systems, -1, width)
    picked = jnp.take(grouped, block_cols, axis=1)
    products = jnp.einsum("kij,nkj->nki", blocks, picked, precision=lax.Precision.HIGHEST)
    own_rows = lax.psum_scatter(
        jnp.einsum("mk,nki->mni", rows_onehot, products, precision=lax.Precision.HIGHEST),
        "col",
        scatter_dimension=0,
        tiled=True,
    )
    summed = jnp.transpose(own_rows, (1, 0, 2)).reshape(systems, -1)
    return diagonal[None, :] * vector + summed


def body(blocks, block_rows, block_cols, diagonal, right_sides):
    systems = right_sides.shape[0]
    width = blocks.shape[1]
    row_count = lax.axis_size("col") * (right_sides.shape[1] // width)
    positions = jnp.arange(row_count, dtype=jnp.int32)
    rows_onehot = (block_rows[0][None, :] == positions[:, None]).astype(jnp.float32)
    columns_local = block_cols[0]
    total_steps = STEPS
    initial_norm = jnp.sqrt(
        lax.psum(jnp.sum(right_sides * right_sides, axis=1), ("row", "col")) + epsilon
    )
    krylov_basis = [right_sides / initial_norm[:, None]]
    hessenberg = jnp.zeros((systems, total_steps + 1, total_steps), jnp.float32)
    for j in range(total_steps):
        candidate = apply_matrix(krylov_basis[j], blocks, rows_onehot, columns_local, diagonal)
        stacked = jnp.stack(krylov_basis)
        local_dots = jnp.einsum("inl,nl->ni", stacked, candidate, precision=lax.Precision.HIGHEST)
        coeffs = lax.psum(local_dots, ("row", "col"))
        candidate = candidate - jnp.einsum(
            "ni,inl->nl", coeffs, stacked, precision=lax.Precision.HIGHEST
        )
        remainder_sq = lax.psum(jnp.sum(candidate * candidate, axis=1), ("row", "col"))
        new_norm = jnp.sqrt(remainder_sq + epsilon)
        hessenberg = hessenberg.at[:, : j + 1, j].set(coeffs)
        hessenberg = hessenberg.at[:, j + 1, j].set(new_norm)
        krylov_basis.append(candidate / new_norm[:, None])
    weights = least_squares(hessenberg, initial_norm)
    solution = jnp.einsum(
        "ni,inl->nl",
        weights,
        jnp.stack(krylov_basis[:total_steps]),
        precision=lax.Precision.HIGHEST,
    )
    return (solution, hessenberg)


def solution(mesh):
    return jax.shard_map(
        body,
        mesh=mesh,
        in_specs=(
            P(("row", "col"), None, None),
            P(("row", "col"), None),
            P(("row", "col"), None),
            P(("row", "col")),
            P(None, ("row", "col")),
        ),
        out_specs=(P(None, ("row", "col")), P()),
        check_vma=False,
    )
```

profile of v0, /device:TPU:0, one launch (start us, length us, event | category | flops | bytes accessed | tf_op | source)
XLA Modules:
  0.0 1472.0 jit_solution(12052770710032486379)
XLA Ops:
  9.7 41.9 %psum.119 = f32[2]{0:T(128)S(1)} all-reduce(f32[2]{0:T(128)S(1)} %multiply_reduce_fusion.8), channel_id=1, replica_groups=mesh['row'=4,'col'=8] {'row','col'}, use_global_device_ids=true, to_apply=%region_1.0 | all-reduce | flops 2 | bytes 16 | tf_op jit(solution)/shard_map/psum | solution.py:64
  52.7 7.9 all_gather.24
  61.4 15.5 %convolution_bitcast_fusion.7 = f32[2,128,128]{2,0,1:T(2,128)S(1)} fusion(f32[128,128,128]{2,1,0:T(8,128)} %param.39, f32[128,2,128]{2,1,0:T(2,128)S(1)} %gather_fusion, pred[128]{0:T(512)(128)(4,1)S(1)} %compare_and_fusion), kind=kOutput, calls=%fused_computation.19 | convolution fusion | flops 50364416 | bytes 8650880 | tf_op jit(solution)/shard_map/kij,nkj->nki/dot_general | solution.py:44
  79.3 62.7 %reduce-scatter.9.cloned.1.call-done = f32[128,2,128]{2,0,1:T(8,128)} async-done(((f32[1024,2,128]{2,0,1:T(8,128)}), f32[128,2,128]{2,0,1:T(8,128)}) %reduce-scatter.9.cloned.1.call-update) | async-done | bytes 131088 | tf_op jit(solution)/shard_map/reduce_scatter | solution.py:45
  143.1 39.9 %psum.120 = f32[2,1]{0,1:T(1,128)S(1)} all-reduce(f32[2,1]{0,1:T(1,128)S(1)} %bitcast.742), channel_id=1, replica_groups=mesh['row'=4,'col'=8] {'row','col'}, use_global_device_ids=true, to_apply=%region_3.5 | all-reduce | flops 2 | bytes 16 | tf_op jit(solution)/shard_map/psum | solution.py:72
  184.2 39.2 %psum.121 = f32[2]{0:T(128)S(1)} all-reduce(f32[2]{0:T(128)S(1)} %get-tuple-element.266), channel_id=1, replica_groups=mesh['row'=4,'col'=8] {'row','col'}, use_global_device_ids=true, to_apply=%region_5.7 | all-reduce | flops 2 | bytes 16 | tf_op jit(solution)/shard_map/psum | solution.py:76
  223.6 8.1 all_gather.25
  232.5 15.5 %convolution_bitcast_fusion.6 = f32[2,128,128]{2,0,1:T(2,128)S(1)} fusion(f32[128,128,128]{2,1,0:T(8,128)} %param.39, f32[128,2,128]{2,1,0:T(2,128)S(1)} %gather_fusion.1, pred[128]{0:T(512)(128)(4,1)S(1)} %compare_and_fusion), kind=kOutput, calls=%fused_computation.18 | convolution fusion | flops 50364416 | bytes 8650880 | tf_op jit(solution)/shard_map/kij,nkj->nki/dot_general | solution.py:44
  251.0 61.7 %reduce-scatter.11.cloned.1.call-done = f32[128,2,128]{2,0,1:T(8,128)} async-done(((f32[1024,2,128]{2,0,1:T(8,128)}), f32[128,2,128]{2,0,1:T(8,128)}) %reduce-scatter.11.cloned.1.call-update) | async-done | bytes 131088 | tf_op jit(solution)/shard_map/reduce_scatter | solution.py:45
  313.8 2.5 fusion.53
  316.2 39.8 %psum.122 = f32[2,2]{1,0:T(2,128)S(1)} all-reduce(f32[2,2]{1,0:T(2,128)S(1)} %bitcast.732), channel_id=1, replica_groups=mesh['row'=4,'col'=8] {'row','col'}, use_global_device_ids=true, to_apply=%region_7.9 | all-reduce | flops 4 | bytes 32 | tf_op jit(solution)/shard_map/psum | solution.py:72
  357.4 39.2 %psum.123 = f32[2]{0:T(128)S(1)} all-reduce(f32[2]{0:T(128)S(1)} %multiply_reduce_fusion.6), channel_id=1, replica_groups=mesh['row'=4,'col'=8] {'row','col'}, use_global_device_ids=true, to_apply=%region_9.11 | all-reduce | flops 2 | bytes 16 | tf_op jit(solution)/shard_map/psum | solution.py:76
  396.8 8.2 all_gather.26
  406.4 15.5 %convolution_bitcast_fusion.5 = f32[2,128,128]{2,0,1:T(2,128)S(1)} fusion(f32[128,128,128]{2,1,0:T(8,128)} %param.39, f32[128,2,128]{2,1,0:T(2,128)} %gather_fusion.2, pred[128]{0:T(512)(128)(4,1)S(1)} %compare_and_fusion), kind=kOutput, calls=%fused_computation.17 | convolution fusion | flops 50364416 | bytes 8650880 | tf_op jit(solution)/shard_map/kij,nkj->nki/dot_general | solution.py:44
  425.1 61.8 %reduce-scatter.13.cloned.1.call-done = f32[128,2,128]{2,0,1:T(8,128)} async-done(((f32[1024,2,128]{2,0,1:T(8,128)}), f32[128,2,128]{2,0,1:T(8,128)}) %reduce-scatter.13.cloned.1.call-update) | async-done | bytes 131088 | tf_op jit(solution)/shard_map/reduce_scatter | solution.py:45
  487.9 2.5 fusion.20
  490.4 39.8 %psum.124 = f32[2,3]{1,0:T(2,128)S(1)} all-reduce(f32[2,3]{1,0:T(2,128)S(1)} %bitcast.733), channel_id=1, replica_groups=mesh['row'=4,'col'=8] {'row','col'}, use_global_device_ids=true, to_apply=%region_12.14 | all-reduce | flops 6 | bytes 48 | tf_op jit(solution)/shard_map/psum | solution.py:72
  532.7 39.2 %psum.125 = f32[2]{0:T(128)S(1)} all-reduce(f32[2]{0:T(128)S(1)} %multiply_reduce_fusion.5), channel_id=1, replica_groups=mesh['row'=4,'col'=8] {'row','col'}, use_global_device_ids=true, to_apply=%region_14.16 | all-reduce | flops 2 | bytes 16 | tf_op jit(solution)/shard_map/psum | solution.py:76
  573.0 8.8 all_gather.27
  583.6 15.5 %convolution_bitcast_fusion.4 = f32[2,128,128]{2,0,1:T(2,128)S(1)} fusion(f32[128,128,128]{2,1,0:T(8,128)} %param.39, f32[128,2,128]{2,1,0:T(2,128)S(1)} %gather_fusion.3, pred[128]{0:T(512)(128)(4,1)S(1)} %compare_and_fusion), kind=kOutput, calls=%fused_computation.16 | convolution fusion | flops 50364416 | bytes 8650880 | tf_op jit(solution)/shard_map/kij,nkj->nki/dot_general | solution.py:44
  602.6 61.4 %reduce-scatter.15.cloned.1.call-done = f32[128,2,128]{2,0,1:T(8,128)} async-done(((f32[1024,2,128]{2,0,1:T(8,128)}), f32[128,2,128]{2,0,1:T(8,128)}) %reduce-scatter.15.cloned.1.call-update) | async-done | bytes 131088 | tf_op jit(solution)/shard_map/reduce_scatter | solution.py:45
  665.0 3.6 fusion.41
  668.6 39.8 %psum.126 = f32[2,4]{1,0:T(2,128)S(1)} all-reduce(f32[2,4]{1,0:T(2,128)S(1)} %bitcast.734), channel_id=1, replica_groups=mesh['row'=4,'col'=8] {'row','col'}, use_global_device_ids=true, to_apply=%region_17.19 | all-reduce | flops 8 | bytes 64 | tf_op jit(solution)/shard_map/psum | solution.py:72
  712.2 39.1 %psum.127 = f32[2]{0:T(128)S(1)} all-reduce(f32[2]{0:T(128)S(1)} %multiply_reduce_fusion.4), channel_id=1, replica_groups=mesh['row'=4,'col'=8] {'row','col'}, use_global_device_ids=true, to_apply=%region_19.21 | all-reduce | flops 2 | bytes 16 | tf_op jit(solution)/shard_map/psum | solution.py:76
  753.1 8.6 all_gather.28
  764.1 15.5 %convolution_bitcast_fusion.3 = f32[2,128,128]{2,0,1:T(2,128)S(1)} fusion(f32[128,128,128]{2,1,0:T(8,128)} %param.39, f32[128,2,128]{2,1,0:T(2,128)} %gather_fusion.4, pred[128]{0:T(512)(128)(4,1)S(1)} %compare_and_fusion), kind=kOutput, calls=%fused_computation.15 | convolution fusion | flops 50364416 | bytes 8650880 | tf_op jit(solution)/shard_map/kij,nkj->nki/dot_general | solution.py:44
  782.3 62.2 %reduce-scatter.17.cloned.1.call-done = f32[128,2,128]{2,0,1:T(8,128)} async-done(((f32[1024,2,128]{2,0,1:T(8,128)}), f32[128,2,128]{2,0,1:T(8,128)}) %reduce-scatter.17.cloned.1.call-update) | async-done | bytes 131088 | tf_op jit(solution)/shard_map/reduce_scatter | solution.py:45
  846.3 2.6 fusion.2
  848.9 39.8 %psum.128 = f32[2,5]{1,0:T(2,128)S(1)} all-reduce(f32[2,5]{1,0:T(2,128)S(1)} %bitcast.727), channel_id=1, replica_groups=mesh['row'=4,'col'=8] {'row','col'}, use_global_device_ids=true, to_apply=%region_22.24 | all-reduce | flops 10 | bytes 80 | tf_op jit(solution)/shard_map/psum | solution.py:72
  891.8 39.3 %psum.129 = f32[2]{0:T(128)S(1)} all-reduce(f32[2]{0:T(128)S(1)} %multiply_reduce_fusion.3), channel_id=1, replica_groups=mesh['row'=4,'col'=8] {'row','col'}, use_global_device_ids=true, to_apply=%region_24.26 | all-reduce | flops 2 | bytes 16 | tf_op jit(solution)/shard_map/psum | solution.py:76
  932.3 8.2 all_gather.29
  941.8 15.5 %convolution_bitcast_fusion.2 = f32[2,128,128]{2,0,1:T(2,128)S(1)} fusion(f32[128,128,128]{2,1,0:T(8,128)} %param.39, f32[128,2,128]{2,1,0:T(2,128)} %gather_fusion.5, pred[128]{0:T(512)(128)(4,1)S(1)} %compare_and_fusion), kind=kOutput, calls=%fused_computation.14 | convolution fusion | flops 50364416 | bytes 8650880 | tf_op jit(solution)/shard_map/kij,nkj->nki/dot_general | solution.py:44
  959.1 63.2 %reduce-scatter.19.cloned.1.call-done = f32[128,2,128]{2,0,1:T(8,128)} async-done(((f32[1024,2,128]{2,0,1:T(8,128)}), f32[128,2,128]{2,0,1:T(8,128)}) %reduce-scatter.19.cloned.1.call-update) | async-done | bytes 131088 | tf_op jit(solution)/shard_map/reduce_scatter | solution.py:45
  1023.3 2.9 fusion.6
  1026.2 39.8 %psum.130 = f32[2,6]{1,0:T(2,128)S(1)} all-reduce(f32[2,6]{1,0:T(2,128)S(1)} %bitcast.728), channel_id=1, replica_groups=mesh['row'=4,'col'=8] {'row','col'}, use_global_device_ids=true, to_apply=%region_27.29 | all-reduce | flops 12 | bytes 96 | tf_op jit(solution)/shard_map/psum | solution.py:72
  1068.3 39.2 %psum.131 = f32[2]{0:T(128)S(1)} all-reduce(f32[2]{0:T(128)S(1)} %multiply_reduce_fusion.2), channel_id=1, replica_groups=mesh['row'=4,'col'=8] {'row','col'}, use_global_device_ids=true, to_apply=%region_29.31 | all-reduce | flops 2 | bytes 16 | tf_op jit(solution)/shard_map/psum | solution.py:76
  1107.7 8.4 all_gather.30
  1116.8 15.5 %convolution_bitcast_fusion.1 = f32[2,128,128]{2,0,1:T(2,128)S(1)} fusion(f32[128,128,128]{2,1,0:T(8,128)} %param.39, f32[128,2,128]{2,1,0:T(2,128)S(1)} %gather_fusion.6, pred[128]{0:T(512)(128)(4,1)S(1)} %compare_and_fusion), kind=kOutput, calls=%fused_computation.13 | convolution fusion | flops 50364416 | bytes 8650880 | tf_op jit(solution)/shard_map/kij,nkj->nki/dot_general | solution.py:44
  1134.0 63.2 %reduce-scatter.21.cloned.1.call-done = f32[128,2,128]{2,0,1:T(8,128)} async-done(((f32[1024,2,128]{2,0,1:T(8,128)}), f32[128,2,128]{2,0,1:T(8,128)}) %reduce-scatter.21.cloned.1.call-update) | async-done | bytes 131088 | tf_op jit(solution)/shard_map/reduce_scatter | solution.py:45
  1198.3 2.9 fusion.10
  1201.2 39.9 %psum.132 = f32[2,7]{1,0:T(2,128)S(1)} all-reduce(f32[2,7]{1,0:T(2,128)S(1)} %bitcast.729), channel_id=1, replica_groups=mesh['row'=4,'col'=8] {'row','col'}, use_global_device_ids=true, to_apply=%region_32.34 | all-reduce | flops 14 | bytes 112 | tf_op jit(solution)/shard_map/psum | solution.py:72
  1242.8 39.2 %psum.133 = f32[2]{0:T(128)S(1)} all-reduce(f32[2]{0:T(128)S(1)} %multiply_reduce_fusion.1), channel_id=1, replica_groups=mesh['row'=4,'col'=8] {'row','col'}, use_global_device_ids=true, to_apply=%region_34.36 | all-reduce | flops 2 | bytes 16 | tf_op jit(solution)/shard_map/psum | solution.py:76
  1282.2 8.1 all_gather.31
  1291.1 15.5 %convolution_bitcast_fusion = f32[2,128,128]{2,0,1:T(2,128)S(1)} fusion(f32[128,128,128]{2,1,0:T(8,128)} %param.39, f32[128,2,128]{2,1,0:T(2,128)S(1)} %gather_fusion.7, pred[128]{0:T(512)(128)(4,1)S(1)} %compare_and_fusion), kind=kOutput, calls=%fused_computation.12 | convolution fusion | flops 50364416 | bytes 8650880 | tf_op jit(solution)/shard_map/kij,nkj->nki/dot_general | solution.py:44
  1332.2 39.3 %reduce-scatter.23.cloned.1.call-done = f32[128,2,128]{2,0,1:T(8,128)} async-done(((f32[1024,2,128]{2,0,1:T(8,128)}), f32[128,2,128]{2,0,1:T(8,128)}) %reduce-scatter.23.cloned.1.call-update) | async-done | bytes 131088 | tf_op jit(solution)/shard_map/reduce_scatter | solution.py:45
  1372.6 3.0 fusion.16
  1375.6 39.8 %psum.134 = f32[2,8]{1,0:T(2,128)S(1)} all-reduce(f32[2,8]{1,0:T(2,128)S(1)} %bitcast.726), channel_id=1, replica_groups=mesh['row'=4,'col'=8] {'row','col'}, use_global_device_ids=true, to_apply=%region_37.39 | all-reduce | flops 16 | bytes 128 | tf_op jit(solution)/shard_map/psum | solution.py:72
  1418.4 39.2 %psum.135 = f32[2]{0:T(128)S(1)} all-reduce(f32[2]{0:T(128)S(1)} %fusion.56), channel_id=1, replica_groups=mesh['row'=4,'col'=8] {'row','col'}, use_global_device_ids=true, to_apply=%region_39.41 | all-reduce | flops 2 | bytes 16 | tf_op jit(solution)/shard_map/psum | solution.py:76
  (181 shorter events, 97.4 us)
Async XLA Ops:
  7.2 69.7 %copy-start.8 = (s32[1,128]{1,0:T(1,128)S(1)}, s32[1,128]{1,0:T(1,128)}, u32[]{:S(2)}) copy-start(s32[1,128]{1,0:T(1,128)} %param.40) | copy-start | bytes 1540
  7.2 134.8 %copy-start = (f32[16384]{0:T(1024)S(1)}, f32[16384]{0:T(1024)}, u32[]{:S(2)}) copy-start(f32[16384]{0:T(1024)} %param.42) | copy-start | bytes 196612
  7.2 134.8 %reduce-scatter.9.cloned.1.call-start = ((), (), s32[]{:S(2)}) async-start(), calls=%async_computation.8 | async-start | bytes 1179648 | tf_op jit(solution)/shard_map/reduce_scatter | solution.py:45
  78.5 234.2 %reduce-scatter.11.cloned.1.call-start = ((), (), s32[]{:S(2)}) async-start(), calls=%async_computation.9 | async-start | bytes 1179648 | tf_op jit(solution)/shard_map/reduce_scatter | solution.py:45
  249.6 237.3 %reduce-scatter.13.cloned.1.call-start = ((), (), s32[]{:S(2)}) async-start(), calls=%async_computation.10 | async-start | bytes 1179648 | tf_op jit(solution)/shard_map/reduce_scatter | solution.py:45
  423.5 240.4 %reduce-scatter.15.cloned.1.call-start = ((), (), s32[]{:S(2)}) async-start(), calls=%async_computation.11 | async-start | bytes 1179648 | tf_op jit(solution)/shard_map/reduce_scatter | solution.py:45
  531.3 0.7 copy-start.6
  600.7 243.8 %reduce-scatter.17.cloned.1.call-start = ((), (), s32[]{:S(2)}) async-start(), calls=%async_computation.12 | async-start | bytes 1179648 | tf_op jit(solution)/shard_map/reduce_scatter | solution.py:45
  665.0 46.0 %copy-start.4 = (f32[2,16384]{1,0:T(2,128)}, f32[2,16384]{1,0:T(2,128)S(1)}, u32[]{:S(2)}) copy-start(f32[2,16384]{1,0:T(2,128)S(1)} %bitcast_add_fusion.4) | copy-start | bytes 393220
  710.8 0.6 copy-start.5
  712.2 69.1 %copy-start.1 = (f32[7,2,16384]{2,1,0:T(2,128)S(1)}, f32[7,2,16384]{2,1,0:T(2,128)}, u32[]{:S(2)}) copy-start(f32[7,2,16384]{2,1,0:T(2,128)} %get-tuple-element.273) | copy-start | bytes 2752516
  752.5 0.7 copy-start.2
  781.2 241.0 %reduce-scatter.19.cloned.1.call-start = ((), (), s32[]{:S(2)}) async-start(), calls=%async_computation.13 | async-start | bytes 1179648 | tf_op jit(solution)/shard_map/reduce_scatter | solution.py:45
  845.6 0.7 copy-start.3
  890.0 0.6 copy-start.7
  958.9 238.3 %reduce-scatter.21.cloned.1.call-start = ((), (), s32[]{:S(2)}) async-start(), calls=%async_computation.14 | async-start | bytes 1179648 | tf_op jit(solution)/shard_map/reduce_scatter | solution.py:45
  1133.8 175.5 %copy-start.14 = (s32[3]{0:T(128)S(1)}, s32[3]{0:T(128)}, u32[]{:S(2)}) copy-start(s32[3]{0:T(128)} %constant.460.clone.1) | copy-start | bytes 40
  1133.9 176.2 %copy-start.13 = (s32[3]{0:T(128)S(1)}, s32[3]{0:T(128)}, u32[]{:S(2)}) copy-start(s32[3]{0:T(128)} %constant.463.clone.1) | copy-start | bytes 40
  1133.9 177.0 %copy-start.12 = (s32[3]{0:T(128)S(1)}, s32[3]{0:T(128)}, u32[]{:S(2)}) copy-start(s32[3]{0:T(128)} %constant.465.clone.1) | copy-start | bytes 40
  1133.9 177.7 %copy-start.11 = (s32[3]{0:T(128)S(1)}, s32[3]{0:T(128)}, u32[]{:S(2)}) copy-start(s32[3]{0:T(128)} %constant.467.clone.1) | copy-start | bytes 40
  1133.9 178.5 %copy-start.10 = (s32[3]{0:T(128)S(1)}, s32[3]{0:T(128)}, u32[]{:S(2)}) copy-start(s32[3]{0:T(128)} %constant.469.clone.1) | copy-start | bytes 40
  1133.9 179.2 %copy-start.9 = (s32[3]{0:T(128)S(1)}, s32[3]{0:T(128)}, u32[]{:S(2)}) copy-start(s32[3]{0:T(128)} %constant.471.clone.1) | copy-start | bytes 40
  1133.9 237.6 %reduce-scatter.23.cloned.1.call-start = ((), (), s32[]{:S(2)}) async-start(), calls=%async_computation.15 | async-start | bytes 1179648 | tf_op jit(solution)/shard_map/reduce_scatter | solution.py:45
Sparse Core Ops, SparseCore 0:
  78.6 63.3 reduce-scatter.8
  249.7 62.9 reduce-scatter.10
  423.6 63.1 reduce-scatter.12
  600.8 63.0 reduce-scatter.14
  781.3 63.1 reduce-scatter.16
  959.1 63.1 reduce-scatter.18
  1134.0 63.1 reduce-scatter.20
  1308.3 63.1 reduce-scatter.22
where the time goes:
time: 1480 us; the launch traced here: 1470 us
  blocking collectives  740 us (50%)
  waiting for transfers between devices  476 us (32%)
  matrix products  168 us (11%)
  other arithmetic  38.8 us (3%)
  local copies, waits for them, and re-layouts  33.9 us (2%)
  between operations  14.8 us (1%)
    reduce_scatter x8, waiting for transfers between devices, apply_matrix(): lax.psum_scatter(jnp.einsum('mk,nki->mni', rows_onehot, products, precisi...  475 us
    psum x8, blocking collectives, body(): coeffs = lax.psum(local_dots, ('row', 'col'))  319 us
    psum x8, blocking collectives, body(): lax.psum(jnp.sum(candidate * candidate, axis=1), ('row', 'col'))  314 us
    dot_general x8, matrix products, apply_matrix(): jnp.einsum('kij,nkj->nki', blocks, picked, precision=lax.Precision.HIGHEST)  124 us
    all_gather x8, blocking collectives, apply_matrix(): gathered = lax.all_gather(vector, 'row', axis=1, tiled=True)  66.2 us
    psum x1, blocking collectives, body(): lax.psum(jnp.sum(right_sides * right_sides, axis=1), ('row', 'col'))  41.9 us
  transfers between devices with their start and end apart: 8, of which 8 were waited for; matrix products, arithmetic and copies ran while one was open for 2% of the time, Pallas kernels for 0%

commit v1 on v0

--- a/solution.py
+++ b/solution.py
@@ -73,7 +73,7 @@
         candidate = candidate - jnp.einsum(
             "ni,inl->nl", coeffs, stacked, precision=lax.Precision.HIGHEST
         )
-        remainder_sq = lax.psum(jnp.sum(candidate * candidate, axis=1), ("row", "col"))
+        remainder_sq = lax.psum(lax.psum(jnp.sum(candidate * candidate, axis=1), "row"), "col")
         new_norm = jnp.sqrt(remainder_sq + epsilon)
         hessenberg = hessenberg.at[:, : j + 1, j].set(coeffs)
         hessenberg = hessenberg.at[:, j + 1, j].set(new_norm)

time: 1480 us -> 1350 us (0.912)
  blocking collectives: 740 us -> 626 us
    psum x8 -> x16, blocking collectives: 314 us -> 210 us  [the longest x8 164 us: body(): lax.psum(lax.psum(jnp.sum(candidate * candidate, axis=1), 'row'), 'col')]
where the time goes in v1:
time: 1350 us; the launch traced here: 1340 us
  blocking collectives  626 us (46%)
  waiting for transfers between devices  466 us (35%)
  matrix products  169 us (13%)
  other arithmetic  36.5 us (3%)
  local copies, waits for them, and re-layouts  28 us (2%)
  between operations  14.7 us (1%)
    reduce_scatter x8, waiting for transfers between devices, apply_matrix(): lax.psum_scatter(jnp.einsum('mk,nki->mni', rows_onehot, products, precisi...  466 us
    psum x8, blocking collectives, body(): coeffs = lax.psum(local_dots, ('row', 'col'))  319 us
    psum x8, blocking collectives, body(): lax.psum(lax.psum(jnp.sum(candidate * candidate, axis=1), 'row'), 'col')  164 us
    dot_general x8, matrix products, apply_matrix(): jnp.einsum('kij,nkj->nki', blocks, picked, precision=lax.Precision.HIGHEST)  124 us
    all_gather x8, blocking collectives, apply_matrix(): gathered = lax.all_gather(vector, 'row', axis=1, tiled=True)  55.7 us
    psum x8, blocking collectives, body(): lax.psum(jnp.sum(candidate * candidate, axis=1), 'row')  46.4 us
    psum x1, blocking collectives, body(): lax.psum(jnp.sum(right_sides * right_sides, axis=1), ('row', 'col'))  41.9 us
  transfers between devices with their start and end apart: 8, of which 8 were waited for; matrix products, arithmetic and copies ran while one was open for 2% of the time, Pallas kernels for 0%

profile of v1, /device:TPU:0, one launch (start us, length us, event | category | flops | bytes accessed | tf_op | source)
XLA Modules:
  0.0 1340.4 jit_solution(7146938113595902983)
XLA Ops:
  9.7 41.9 %psum.175 = f32[2]{0:T(128)S(1)} all-reduce(f32[2]{0:T(128)S(1)} %multiply_reduce_fusion.8), channel_id=1, replica_groups=mesh['row'=4,'col'=8] {'row','col'}, use_global_device_ids=true, to_apply=%region_1.0 | all-reduce | flops 2 | bytes 16 | tf_op jit(solution)/shard_map/psum | solution.py:64
  52.7 7.9 all_gather.24
  61.4 15.5 %convolution_bitcast_fusion.7 = f32[2,128,128]{2,0,1:T(2,128)S(1)} fusion(f32[128,128,128]{2,1,0:T(8,128)} %param.39, f32[128,2,128]{2,1,0:T(2,128)S(1)} %gather_fusion, pred[128]{0:T(512)(128)(4,1)S(1)} %compare_and_fusion), kind=kOutput, calls=%fused_computation.19 | convolution fusion | flops 50364416 | bytes 8650880 | tf_op jit(solution)/shard_map/kij,nkj->nki/dot_general | solution.py:44
  78.5 63.3 %reduce-scatter.9.cloned.1.call-done = f32[128,2,128]{2,0,1:T(8,128)} async-done(((f32[1024,2,128]{2,0,1:T(8,128)}), f32[128,2,128]{2,0,1:T(8,128)}) %reduce-scatter.9.cloned.1.call-update) | async-done | bytes 131088 | tf_op jit(solution)/shard_map/reduce_scatter | solution.py:45
  142.9 39.9 %psum.176 = f32[2,1]{0,1:T(1,128)S(1)} all-reduce(f32[2,1]{0,1:T(1,128)S(1)} %bitcast.742), channel_id=1, replica_groups=mesh['row'=4,'col'=8] {'row','col'}, use_global_device_ids=true, to_apply=%region_3.5 | all-reduce | flops 2 | bytes 16 | tf_op jit(solution)/shard_map/psum | solution.py:72
  184.0 5.8 psum.177
  189.8 20.6 %psum.178 = f32[2]{0:T(128)S(1)} all-reduce(f32[2]{0:T(128)S(1)} %psum.177), channel_id=1, replica_groups=mesh['row'=4,'col'=8] {'col'}, use_global_device_ids=true, to_apply=%region_6.8 | all-reduce | flops 2 | bytes 16 | tf_op jit(solution)/shard_map/psum | solution.py:76
  210.6 6.7 all_gather.25
  218.0 15.5 %convolution_bitcast_fusion.6 = f32[2,128,128]{2,0,1:T(2,128)S(1)} fusion(f32[128,128,128]{2,1,0:T(8,128)} %param.39, f32[128,2,128]{2,1,0:T(2,128)S(1)} %gather_fusion.1, pred[128]{0:T(512)(128)(4,1)S(1)} %compare_and_fusion), kind=kOutput, calls=%fused_computation.18 | convolution fusion | flops 50364416 | bytes 8650880 | tf_op jit(solution)/shard_map/kij,nkj->nki/dot_general | solution.py:44
  235.3 61.1 %reduce-scatter.11.cloned.1.call-done = f32[128,2,128]{2,0,1:T(8,128)} async-done(((f32[1024,2,128]{2,0,1:T(8,128)}), f32[128,2,128]{2,0,1:T(8,128)}) %reduce-scatter.11.cloned.1.call-update) | async-done | bytes 131088 | tf_op jit(solution)/shard_map/reduce_scatter | solution.py:45
  299.9 39.8 %psum.179 = f32[2,2]{1,0:T(2,128)S(1)} all-reduce(f32[2,2]{1,0:T(2,128)S(1)} %bitcast.732), channel_id=1, replica_groups=mesh['row'=4,'col'=8] {'row','col'}, use_global_device_ids=true, to_apply=%region_8.10 | all-reduce | flops 4 | bytes 32 | tf_op jit(solution)/shard_map/psum | solution.py:72
  341.1 5.8 psum.180
  346.9 20.2 %psum.181 = f32[2]{0:T(128)S(1)} all-reduce(f32[2]{0:T(128)S(1)} %psum.180), channel_id=1, replica_groups=mesh['row'=4,'col'=8] {'col'}, use_global_device_ids=true, to_apply=%region_11.13 | all-reduce | flops 2 | bytes 16 | tf_op jit(solution)/shard_map/psum | solution.py:76
  367.3 6.7 all_gather.26
  374.8 15.5 %convolution_bitcast_fusion.5 = f32[2,128,128]{2,0,1:T(2,128)S(1)} fusion(f32[128,128,128]{2,1,0:T(8,128)} %param.39, f32[128,2,128]{2,1,0:T(2,128)S(1)} %gather_fusion.2, pred[128]{0:T(512)(128)(4,1)S(1)} %compare_and_fusion), kind=kOutput, calls=%fused_computation.17 | convolution fusion | flops 50364416 | bytes 8650880 | tf_op jit(solution)/shard_map/kij,nkj->nki/dot_general | solution.py:44
  393.4 59.7 %reduce-scatter.13.cloned.1.call-done = f32[128,2,128]{2,0,1:T(8,128)} async-done(((f32[1024,2,128]{2,0,1:T(8,128)}), f32[128,2,128]{2,0,1:T(8,128)}) %reduce-scatter.13.cloned.1.call-update) | async-done | bytes 131088 | tf_op jit(solution)/shard_map/reduce_scatter | solution.py:45
  456.7 39.8 %psum.182 = f32[2,3]{1,0:T(2,128)S(1)} all-reduce(f32[2,3]{1,0:T(2,128)S(1)} %bitcast.733), channel_id=1, replica_groups=mesh['row'=4,'col'=8] {'row','col'}, use_global_device_ids=true, to_apply=%region_14.16 | all-reduce | flops 6 | bytes 48 | tf_op jit(solution)/shard_map/psum | solution.py:72
  500.1 5.8 psum.183
  505.9 20.6 %psum.184 = f32[2]{0:T(128)S(1)} all-reduce(f32[2]{0:T(128)S(1)} %psum.183), channel_id=1, replica_groups=mesh['row'=4,'col'=8] {'col'}, use_global_device_ids=true, to_apply=%region_17.19 | all-reduce | flops 2 | bytes 16 | tf_op jit(solution)/shard_map/psum | solution.py:76
  527.6 7.4 all_gather.27
  536.7 15.5 %convolution_bitcast_fusion.4 = f32[2,128,128]{2,0,1:T(2,128)S(1)} fusion(f32[128,128,128]{2,1,0:T(8,128)} %param.39, f32[128,2,128]{2,1,0:T(2,128)S(1)} %gather_fusion.3, pred[128]{0:T(512)(128)(4,1)S(1)} %compare_and_fusion), kind=kOutput, calls=%fused_computation.16 | convolution fusion | flops 50364416 | bytes 8650880 | tf_op jit(solution)/shard_map/kij,nkj->nki/dot_general | solution.py:44
  555.7 59.5 %reduce-scatter.15.cloned.1.call-done = f32[128,2,128]{2,0,1:T(8,128)} async-done(((f32[1024,2,128]{2,0,1:T(8,128)}), f32[128,2,128]{2,0,1:T(8,128)}) %reduce-scatter.15.cloned.1.call-update) | async-done | bytes 131088 | tf_op jit(solution)/shard_map/reduce_scatter | solution.py:45
  619.8 39.8 %psum.185 = f32[2,4]{1,0:T(2,128)S(1)} all-reduce(f32[2,4]{1,0:T(2,128)S(1)} %bitcast.734), channel_id=1, replica_groups=mesh['row'=4,'col'=8] {'row','col'}, use_global_device_ids=true, to_apply=%region_20.22 | all-reduce | flops 8 | bytes 64 | tf_op jit(solution)/shard_map/psum | solution.py:72
  669.5 20.5 %psum.187 = f32[2]{0:T(128)S(1)} all-reduce(f32[2]{0:T(128)S(1)} %psum.186), channel_id=1, replica_groups=mesh['row'=4,'col'=8] {'col'}, use_global_device_ids=true, to_apply=%region_23.25 | all-reduce | flops 2 | bytes 16 | tf_op jit(solution)/shard_map/psum | solution.py:76
  690.2 6.7 all_gather.28
  697.6 15.5 %convolution_bitcast_fusion.3 = f32[2,128,128]{2,0,1:T(2,128)S(1)} fusion(f32[128,128,128]{2,1,0:T(8,128)} %param.39, f32[128,2,128]{2,1,0:T(2,128)S(1)} %gather_fusion.4, pred[128]{0:T(512)(128)(4,1)S(1)} %compare_and_fusion), kind=kOutput, calls=%fused_computation.15 | convolution fusion | flops 50364416 | bytes 8650880 | tf_op jit(solution)/shard_map/kij,nkj->nki/dot_general | solution.py:44
  715.5 60.5 %reduce-scatter.17.cloned.1.call-done = f32[128,2,128]{2,0,1:T(8,128)} async-done(((f32[1024,2,128]{2,0,1:T(8,128)}), f32[128,2,128]{2,0,1:T(8,128)}) %reduce-scatter.17.cloned.1.call-update) | async-done | bytes 131088 | tf_op jit(solution)/shard_map/reduce_scatter | solution.py:45
  779.7 39.8 %psum.188 = f32[2,5]{1,0:T(2,128)S(1)} all-reduce(f32[2,5]{1,0:T(2,128)S(1)} %bitcast.727), channel_id=1, replica_groups=mesh['row'=4,'col'=8] {'row','col'}, use_global_device_ids=true, to_apply=%region_26.28 | all-reduce | flops 10 | bytes 80 | tf_op jit(solution)/shard_map/psum | solution.py:72
  821.7 5.8 psum.189
  827.5 20.6 %psum.190 = f32[2]{0:T(128)S(1)} all-reduce(f32[2]{0:T(128)S(1)} %psum.189), channel_id=1, replica_groups=mesh['row'=4,'col'=8] {'col'}, use_global_device_ids=true, to_apply=%region_29.31 | all-reduce | flops 2 | bytes 16 | tf_op jit(solution)/shard_map/psum | solution.py:76
  848.3 6.7 all_gather.29
  856.4 15.5 %convolution_bitcast_fusion.2 = f32[2,128,128]{2,0,1:T(2,128)S(1)} fusion(f32[128,128,128]{2,1,0:T(8,128)} %param.39, f32[128,2,128]{2,1,0:T(2,128)} %gather_fusion.5, pred[128]{0:T(512)(128)(4,1)S(1)} %compare_and_fusion), kind=kOutput, calls=%fused_computation.14 | convolution fusion | flops 50364416 | bytes 8650880 | tf_op jit(solution)/shard_map/kij,nkj->nki/dot_general | solution.py:44
  873.7 61.2 %reduce-scatter.19.cloned.1.call-done = f32[128,2,128]{2,0,1:T(8,128)} async-done(((f32[1024,2,128]{2,0,1:T(8,128)}), f32[128,2,128]{2,0,1:T(8,128)}) %reduce-scatter.19.cloned.1.call-update) | async-done | bytes 131088 | tf_op jit(solution)/shard_map/reduce_scatter | solution.py:45
  938.8 39.8 %psum.191 = f32[2,6]{1,0:T(2,128)S(1)} all-reduce(f32[2,6]{1,0:T(2,128)S(1)} %bitcast.728), channel_id=1, replica_groups=mesh['row'=4,'col'=8] {'row','col'}, use_global_device_ids=true, to_apply=%region_32.34 | all-reduce | flops 12 | bytes 96 | tf_op jit(solution)/shard_map/psum | solution.py:72
  980.9 5.8 psum.192
  986.7 20.5 %psum.193 = f32[2]{0:T(128)S(1)} all-reduce(f32[2]{0:T(128)S(1)} %psum.192), channel_id=1, replica_groups=mesh['row'=4,'col'=8] {'col'}, use_global_device_ids=true, to_apply=%region_35.37 | all-reduce | flops 2 | bytes 16 | tf_op jit(solution)/shard_map/psum | solution.py:76
  1007.4 7.0 all_gather.30
  1015.1 15.5 %convolution_bitcast_fusion.1 = f32[2,128,128]{2,0,1:T(2,128)S(1)} fusion(f32[128,128,128]{2,1,0:T(8,128)} %param.39, f32[128,2,128]{2,1,0:T(2,128)S(1)} %gather_fusion.6, pred[128]{0:T(512)(128)(4,1)S(1)} %compare_and_fusion), kind=kOutput, calls=%fused_computation.13 | convolution fusion | flops 50364416 | bytes 8650880 | tf_op jit(solution)/shard_map/kij,nkj->nki/dot_general | solution.py:44
  1032.3 61.2 %reduce-scatter.21.cloned.1.call-done = f32[128,2,128]{2,0,1:T(8,128)} async-done(((f32[1024,2,128]{2,0,1:T(8,128)}), f32[128,2,128]{2,0,1:T(8,128)}) %reduce-scatter.21.cloned.1.call-update) | async-done | bytes 131088 | tf_op jit(solution)/shard_map/reduce_scatter | solution.py:45
  1097.5 39.8 %psum.194 = f32[2,7]{1,0:T(2,128)S(1)} all-reduce(f32[2,7]{1,0:T(2,128)S(1)} %bitcast.729), channel_id=1, replica_groups=mesh['row'=4,'col'=8] {'row','col'}, use_global_device_ids=true, to_apply=%region_38.40 | all-reduce | flops 14 | bytes 112 | tf_op jit(solution)/shard_map/psum | solution.py:72
  1139.7 5.8 psum.195
  1145.5 20.2 %psum.196 = f32[2]{0:T(128)S(1)} all-reduce(f32[2]{0:T(128)S(1)} %psum.195), channel_id=1, replica_groups=mesh['row'=4,'col'=8] {'col'}, use_global_device_ids=true, to_apply=%region_41.43 | all-reduce | flops 2 | bytes 16 | tf_op jit(solution)/shard_map/psum | solution.py:76
  1165.9 6.7 all_gather.31
  1173.4 15.5 %convolution_bitcast_fusion = f32[2,128,128]{2,0,1:T(2,128)S(1)} fusion(f32[128,128,128]{2,1,0:T(8,128)} %param.39, f32[128,2,128]{2,1,0:T(2,128)S(1)} %gather_fusion.7, pred[128]{0:T(512)(128)(4,1)S(1)} %compare_and_fusion), kind=kOutput, calls=%fused_computation.12 | convolution fusion | flops 50364416 | bytes 8650880 | tf_op jit(solution)/shard_map/kij,nkj->nki/dot_general | solution.py:44
  1212.6 39.1 %reduce-scatter.23.cloned.1.call-done = f32[128,2,128]{2,0,1:T(8,128)} async-done(((f32[1024,2,128]{2,0,1:T(8,128)}), f32[128,2,128]{2,0,1:T(8,128)}) %reduce-scatter.23.cloned.1.call-update) | async-done | bytes 131088 | tf_op jit(solution)/shard_map/reduce_scatter | solution.py:45
  1255.8 39.8 %psum.197 = f32[2,8]{1,0:T(2,128)S(1)} all-reduce(f32[2,8]{1,0:T(2,128)S(1)} %bitcast.726), channel_id=1, replica_groups=mesh['row'=4,'col'=8] {'row','col'}, use_global_device_ids=true, to_apply=%region_44.46 | all-reduce | flops 16 | bytes 128 | tf_op jit(solution)/shard_map/psum | solution.py:72
  1299.6 5.8 psum.198
  1305.4 20.6 %psum.199 = f32[2]{0:T(128)S(1)} all-reduce(f32[2]{0:T(128)S(1)} %psum.198), channel_id=1, replica_groups=mesh['row'=4,'col'=8] {'col'}, use_global_device_ids=true, to_apply=%region_47.49 | all-reduce | flops 2 | bytes 16 | tf_op jit(solution)/shard_map/psum | solution.py:76
  (177 shorter events, 115.7 us)
Async XLA Ops:
  7.2 69.7 %copy-start.2 = (s32[1,128]{1,0:T(1,128)S(1)}, s32[1,128]{1,0:T(1,128)}, u32[]{:S(2)}) copy-start(s32[1,128]{1,0:T(1,128)} %param.40) | copy-start | bytes 1540
  7.2 134.6 %copy-start = (f32[16384]{0:T(1024)S(1)}, f32[16384]{0:T(1024)}, u32[]{:S(2)}) copy-start(f32[16384]{0:T(1024)} %param.42) | copy-start | bytes 196612
  7.2 134.6 %reduce-scatter.9.cloned.1.call-start = ((), (), s32[]{:S(2)}) async-start(), calls=%async_computation.8 | async-start | bytes 1179648 | tf_op jit(solution)/shard_map/reduce_scatter | solution.py:45
  78.5 217.9 %reduce-scatter.11.cloned.1.call-start = ((), (), s32[]{:S(2)}) async-start(), calls=%async_computation.9 | async-start | bytes 1179648 | tf_op jit(solution)/shard_map/reduce_scatter | solution.py:45
  235.1 218.1 %reduce-scatter.13.cloned.1.call-start = ((), (), s32[]{:S(2)}) async-start(), calls=%async_computation.10 | async-start | bytes 1179648 | tf_op jit(solution)/shard_map/reduce_scatter | solution.py:45
  391.8 223.3 %reduce-scatter.15.cloned.1.call-start = ((), (), s32[]{:S(2)}) async-start(), calls=%async_computation.11 | async-start | bytes 1179648 | tf_op jit(solution)/shard_map/reduce_scatter | solution.py:45
  553.8 222.2 %reduce-scatter.17.cloned.1.call-start = ((), (), s32[]{:S(2)}) async-start(), calls=%async_computation.12 | async-start | bytes 1179648 | tf_op jit(solution)/shard_map/reduce_scatter | solution.py:45
  714.7 220.1 %reduce-scatter.19.cloned.1.call-start = ((), (), s32[]{:S(2)}) async-start(), calls=%async_computation.13 | async-start | bytes 1179648 | tf_op jit(solution)/shard_map/reduce_scatter | solution.py:45
  820.9 52.7 %copy-start.1 = (f32[7,2,16384]{2,1,0:T(2,128)S(1)}, f32[7,2,16384]{2,1,0:T(2,128)}, u32[]{:S(2)}) copy-start(f32[7,2,16384]{2,1,0:T(2,128)} %get-tuple-element.270) | copy-start | bytes 2752516
  873.5 220.0 %reduce-scatter.21.cloned.1.call-start = ((), (), s32[]{:S(2)}) async-start(), calls=%async_computation.14 | async-start | bytes 1179648 | tf_op jit(solution)/shard_map/reduce_scatter | solution.py:45
  1032.2 159.5 %copy-start.8 = (s32[3]{0:T(128)S(1)}, s32[3]{0:T(128)}, u32[]{:S(2)}) copy-start(s32[3]{0:T(128)} %constant.460.clone.1) | copy-start | bytes 40
  1032.2 160.2 %copy-start.7 = (s32[3]{0:T(128)S(1)}, s32[3]{0:T(128)}, u32[]{:S(2)}) copy-start(s32[3]{0:T(128)} %constant.463.clone.1) | copy-start | bytes 40
  1032.2 160.9 %copy-start.6 = (s32[3]{0:T(128)S(1)}, s32[3]{0:T(128)}, u32[]{:S(2)}) copy-start(s32[3]{0:T(128)} %constant.465.clone.1) | copy-start | bytes 40
  1032.2 161.6 %copy-start.5 = (s32[3]{0:T(128)S(1)}, s32[3]{0:T(128)}, u32[]{:S(2)}) copy-start(s32[3]{0:T(128)} %constant.467.clone.1) | copy-start | bytes 40
  1032.2 162.4 %copy-start.4 = (s32[3]{0:T(128)S(1)}, s32[3]{0:T(128)}, u32[]{:S(2)}) copy-start(s32[3]{0:T(128)} %constant.469.clone.1) | copy-start | bytes 40
  1032.2 163.1 %copy-start.3 = (s32[3]{0:T(128)S(1)}, s32[3]{0:T(128)}, u32[]{:S(2)}) copy-start(s32[3]{0:T(128)} %constant.471.clone.1) | copy-start | bytes 40
  1032.2 219.4 %reduce-scatter.23.cloned.1.call-start = ((), (), s32[]{:S(2)}) async-start(), calls=%async_computation.15 | async-start | bytes 1179648 | tf_op jit(solution)/shard_map/reduce_scatter | solution.py:45
Sparse Core Ops, SparseCore 0:
  78.6 63.1 reduce-scatter.8
  235.2 61.1 reduce-scatter.10
  392.0 61.1 reduce-scatter.12
  553.9 61.2 reduce-scatter.14
  714.8 61.1 reduce-scatter.16
  873.6 61.1 reduce-scatter.18
  1032.4 61.1 reduce-scatter.20
  1190.6 61.0 reduce-scatter.22
